TPU v7x, 32 devices: a whole 2x2x4 slice. The times are simulated.
32 devices in a mesh: ctx: 16 (over z, x, core), head: 2 (over y).
Axes of the slice: x: 2, y: 2, z: 4, core: 2. Of those that a mesh axis runs over, the one named last changes fastest.
Arguments:
- queries: bfloat16 [256, 4096], P('ctx', 'head'), may hold values from -1500 to 1500
- cache_keys: bfloat16 [65536, 2048], P('ctx', 'head'), may hold values from -15 to 15
- prefix_cache_values: bfloat16 [65536, 2048], P('ctx', 'head'), may hold values from -6 to 6
- incoming_keys: bfloat16 [256, 2048], P('ctx', 'head'), may hold values from -15 to 15
- incoming_values: bfloat16 [256, 2048], P('ctx', 'head'), may hold values from -6 to 6
Outputs:
- attended: bfloat16 [256, 4096], P('ctx', 'head')
All inputs are finite; a program needn't handle non-finite values.
Results may differ from a plain program's by a relative error of at most 0.005.
Values may be sent and summed in bfloat16 or wider, within the bound.
A program may use at most 64 MiB of HBM per device.

v0:
```python
import jax
import jax.numpy as jnp
from jax import lax
from jax.sharding import PartitionSpec as P

HEAD_SIZE = 128


score_scale = 168.0 ** (-0.5)


def shards(queries, cache_keys, prefix_cache_values, incoming_keys, incoming_values):
    own_rows = queries.shape[0]
    kv_heads = cache_keys.shape[1] // HEAD_SIZE
    group_size = queries.shape[1] // cache_keys.shape[1]
    gathered = lax.all_gather(queries, "ctx", axis=0, tiled=True)
    fresh_keys, fresh_values = (
        lax.all_gather(incoming_keys, "ctx", axis=0, tiled=True),
        lax.all_gather(incoming_values, "ctx", axis=0, tiled=True),
    )
    total_rows = gathered.shape[0]
    query_heads = gathered.reshape(total_rows, kv_heads, group_size, HEAD_SIZE)
    local_keys = cache_keys.reshape(-1, kv_heads, HEAD_SIZE)
    local_values = prefix_cache_values.reshape(-1, kv_heads, HEAD_SIZE)
    block_size = min(256, local_keys.shape[0])
    count = local_keys.shape[0] // block_size
    blocks = (
        local_keys.reshape(count, block_size, kv_heads, HEAD_SIZE),
        local_values.reshape(count, block_size, kv_heads, HEAD_SIZE),
    )

    def prefix_step(state, key_block):
        out_acc, row_max, row_sum = state
        block_keys, block_values = key_block
        scores = (
            jnp.einsum(
                "qhgd,khd->hgqk", query_heads, block_keys, preferred_element_type=jnp.float32
            )
            * score_scale
        )
        new_max = jnp.maximum(row_max, jnp.max(scores, axis=-1))
        decay = jnp.exp(row_max - new_max)
        probs = jnp.exp(scores - new_max[..., None])
        row_sum = row_sum * decay + jnp.sum(probs, axis=-1)
        contrib = jnp.einsum(
            "hgqk,khd->hgqd",
            probs.astype(jnp.bfloat16),
            block_values,
            preferred_element_type=jnp.float32,
        )
        out_acc = out_acc * decay[..., None] + contrib
        return ((out_acc, new_max, row_sum), None)

    init = (
        jnp.zeros((kv_heads, group_size, total_rows, HEAD_SIZE), jnp.float32),
        jnp.full((kv_heads, group_size, total_rows), -1e30, jnp.float32),
        jnp.zeros((kv_heads, group_size, total_rows), jnp.float32),
    )
    (out_acc, row_max, row_sum), _ = lax.scan(prefix_step, init, blocks)
    own_start = lax.axis_index("ctx") * own_rows
    top_max = lax.pmax(row_max, "ctx")
    rescale = jnp.exp(row_max - top_max)
    prefix_out, prefix_sum = (
        lax.psum_scatter(out_acc * rescale[..., None], "ctx", scatter_dimension=2, tiled=True),
        lax.psum_scatter(row_sum * rescale, "ctx", scatter_dimension=2, tiled=True),
    )
    prefix_max = lax.dynamic_slice_in_dim(top_max, own_start, own_rows, 2)
    own_heads = queries.reshape(own_rows, kv_heads, group_size, HEAD_SIZE)
    fresh_table = fresh_keys.reshape(total_rows, kv_heads, HEAD_SIZE)
    scores = (
        jnp.einsum("qhgd,khd->hgqk", own_heads, fresh_table, preferred_element_type=jnp.float32)
        * score_scale
    )
    query_pos = own_start + jnp.arange(own_rows, dtype=jnp.int32)
    key_pos = jnp.arange(total_rows, dtype=jnp.int32)
    causal_mask = key_pos[None, :] <= query_pos[:, None]
    scores = jnp.where(causal_mask[None, None], scores, -1e30)
    fresh_max = jnp.max(scores, axis=-1)
    fresh_probs = jnp.where(causal_mask[None, None], jnp.exp(scores - fresh_max[..., None]), 0.0)
    fresh_sum = jnp.sum(fresh_probs, axis=-1)
    fresh_out = jnp.einsum(
        "hgqk,khd->hgqd",
        fresh_probs.astype(jnp.bfloat16),
        fresh_values.reshape(total_rows, kv_heads, HEAD_SIZE),
        preferred_element_type=jnp.float32,
    )
    merged_max = jnp.maximum(prefix_max, fresh_max)
    old_weight = jnp.exp(prefix_max - merged_max)
    new_weight = jnp.exp(fresh_max - merged_max)
    numer = prefix_out * old_weight[..., None] + fresh_out * new_weight[..., None]
    denom = prefix_sum * old_weight + fresh_sum * new_weight
    result = (numer / denom[..., None]).transpose(2, 0, 1, 3).reshape(own_rows, -1)
    return result.astype(jnp.bfloat16)


def solution(mesh):
    in_specs = (
        P("ctx", "head"),
        P("ctx", "head"),
        P("ctx", "head"),
        P("ctx", "head"),
        P("ctx", "head"),
    )
    out_specs = P("ctx", "head")
    return jax.shard_map(shards, mesh=mesh, in_specs=in_specs, out_specs=out_specs, check_vma=False)
```

profile of v0, /device:TPU:0, one launch (start us, length us, event | category | flops | bytes accessed | tf_op | source)
XLA Modules:
  0.0 407.7 jit_solution(3803883019437375700)
XLA Ops:
  7.3 8.8 %copy.43 = bf16[512,8,8,128]{3,2,1,0:T(8,128)(2,1)} copy(bf16[512,8,8,128]{3,1,2,0:T(8,128)(2,1)} %bitcast.73) | data formatting | bytes 16777216
  16.1 8.8 %copy.44 = bf16[512,8,8,128]{3,2,1,0:T(8,128)(2,1)} copy(bf16[512,8,8,128]{3,1,2,0:T(8,128)(2,1)} %bitcast.74) | data formatting | bytes 16777216
  24.9 25.2 %all-gather.2.cloned.1.call-done = bf16[256,2048]{1,0:T(8,128)(2,1)} async-done(((bf16[16,2048]{1,0:T(8,128)(2,1)}), bf16[256,2048]{1,0:T(8,128)(2,1)}) %all-gather.2.cloned.1.call-update) | async-done | bytes 1048592 | tf_op jit(solution)/shard_map/all_gather | solution.py:16
  52.9 167.3 %while.15 = (s32[]{:T(128)}, f32[8,2,256,128]{3,2,1,0:T(8,128)S(1)}, f32[8,2,256]{2,1,0:T(2,128)S(1)}, f32[8,2,256]{2,1,0:T(2,128)S(1)}, bf16[16,256,8,128]{3,2,...) while((s32[]{:T(128)}, ...), condition=%wide.region_3.4_spmd.clone, body=%wide.region_0.3_spmd.clone.sunk | while | flops 546852864 | bytes 38011012 | solution.py:59
  54.2 3.9 bitcast_reduce_fusion.2
  64.6 3.9 bitcast_reduce_fusion.2
  75.1 3.9 bitcast_reduce_fusion.2
  85.6 3.9 bitcast_reduce_fusion.2
  96.0 3.9 bitcast_reduce_fusion.2
  106.5 3.9 bitcast_reduce_fusion.2
  116.9 3.9 bitcast_reduce_fusion.2
  127.4 3.9 bitcast_reduce_fusion.2
  137.8 3.9 bitcast_reduce_fusion.2
  148.3 3.9 bitcast_reduce_fusion.2
  158.8 3.9 bitcast_reduce_fusion.2
  169.2 3.9 bitcast_reduce_fusion.2
  179.7 3.9 bitcast_reduce_fusion.2
  190.1 3.9 bitcast_reduce_fusion.2
  200.6 3.9 bitcast_reduce_fusion.2
  220.2 59.7 %pmax.7 = f32[8,2,256]{2,1,0:T(2,128)S(1)} all-reduce(f32[8,2,256]{2,1,0:T(2,128)S(1)} %get-tuple-element.45), channel_id=1, replica_groups=mesh['ctx'=16,'head'=2] {'ctx'}, use_global_device_ids=true, to_apply=%region_4.5 | all-reduce | flops 4096 | bytes 32768 | tf_op jit(solution)/shard_map/pmax | solution.py:61
  283.4 18.7 %all_gather.10 = bf16[256,1024]{1,0:T(8,128)(2,1)S(1)} all-gather(bf16[16,1024]{1,0:T(8,128)(2,1)S(1)} %copy-done.2), channel_id=1, replica_groups=mesh['ctx'=16,'head'=2] {'ctx'}, dimensions={0}, use_global_device_ids=true | all-gather | bytes 557056 | tf_op jit(solution)/shard_map/all_gather | solution.py:18
  302.4 21.0 %all_gather.11 = bf16[256,1024]{1,0:T(8,128)(2,1)S(1)} all-gather(bf16[16,1024]{1,0:T(8,128)(2,1)S(1)} %copy-done.3), channel_id=1, replica_groups=mesh['ctx'=16,'head'=2] {'ctx'}, dimensions={0}, use_global_device_ids=true | all-gather | bytes 557056 | tf_op jit(solution)/shard_map/all_gather | solution.py:19
  324.1 10.4 %reduce-scatter.7.cloned.1.call-done = f32[16,16]{1,0:T(8,128)} async-done(((f32[256,16]{1,0:T(8,128)}), f32[16,16]{1,0:T(8,128)}) %reduce-scatter.7.cloned.1.call-update) | async-done | bytes 1040
  335.6 63.6 %reduce-scatter.5.cloned.1.call-done = f32[8,2,16,128]{3,2,1,0:T(8,128)} async-done(((f32[8,2,256,128]{3,2,1,0:T(8,128)}), f32[8,2,16,128]{3,2,1,0:T(8,128)}) %reduce-scatter.5.cloned.1.call-update) | async-done | bytes 131088 | tf_op jit(solution)/shard_map/reduce_scatter | solution.py:64
  (163 shorter events, 119.5 us)
Async XLA Ops:
  6.5 43.5 %all-gather.2.cloned.1.call-start = ((), (), s32[]{:S(2)}) async-start(), calls=%async_computation.2 | async-start | bytes 1114112 | tf_op jit(solution)/shard_map/all_gather | solution.py:16
  7.3 327.3 %reduce-scatter.7.cloned.1.call-start = ((), (), s32[]{:S(2)}) async-start(), calls=%async_computation.4 | async-start | bytes 139264
  58.0 3.4 copy-start
  68.5 3.4 copy-start
  79.0 3.4 copy-start
  89.4 3.4 copy-start
  99.9 3.4 copy-start
  110.3 3.4 copy-start
  120.8 3.4 copy-start
  131.3 3.4 copy-start
  141.7 3.4 copy-start
  152.2 3.4 copy-start
  162.6 3.4 copy-start
  173.1 3.4 copy-start
  183.6 3.4 copy-start
  194.0 3.4 copy-start
  204.5 3.4 copy-start
  214.9 3.4 copy-start
  279.9 3.5 copy-start.1
  279.9 3.5 copy-start.2
  281.3 21.0 %copy-start.3 = (bf16[16,1024]{1,0:T(8,128)(2,1)S(1)}, bf16[16,1024]{1,0:T(8,128)(2,1)}, u32[]{:S(2)}) copy-start(bf16[16,1024]{1,0:T(8,128)(2,1)} %param.11) | copy-start | bytes 98308
  281.3 117.9 %reduce-scatter.5.cloned.1.call-start = ((), (), s32[]{:S(2)}) async-start(), calls=%async_computation.3 | async-start | bytes 2228224 | tf_op jit(solution)/shard_map/reduce_scatter | solution.py:64
Sparse Core Ops, SparseCore 0:
  9.5 40.5 all-gather.1
  281.5 53.0 reduce-scatter.6
  338.3 60.8 reduce-scatter.4
where the time goes:
time: 409 us; the launch traced here: 408 us
  waiting for transfers between devices  100 us (24%)
  blocking collectives  99.3 us (24%)
  matrix products  92.7 us (23%)
  other arithmetic  52.5 us (13%)
  local copies, waits for them, and re-layouts  49 us (12%)
  between operations  13.3 us (3%)
    reduce_scatter x1, waiting for transfers between devices, shards(): lax.psum_scatter(out_acc * rescale[..., None], 'ctx', scatter_dimension=2...  63.6 us
    dot_general x16, matrix products, prefix_step(): jnp.einsum('qhgd,khd->hgqk', query_heads, block_keys, preferred_element_t...  61.9 us
    pmax x1, blocking collectives, shards(): top_max = lax.pmax(row_max, 'ctx')  59.7 us
    reduce_sum x16, other arithmetic, prefix_step(): row_sum = row_sum * decay + jnp.sum(probs, axis=-1)  49.2 us
    dot_general x16, matrix products, prefix_step(): jnp.einsum('hgqk,khd->hgqd', probs.astype(jnp.bfloat16), block_values, pr...  29.3 us
    all_gather x1, waiting for transfers between devices, shards(): gathered = lax.all_gather(queries, 'ctx', axis=0, tiled=True)  25.2 us
    unnamed x13, local copies, waits for them, and re-layouts  21.2 us
    all_gather x1, blocking collectives, shards(): lax.all_gather(incoming_values, 'ctx', axis=0, tiled=True)  21 us
  transfers between devices with their start and end apart: 3, of which 3 were waited for; matrix products, arithmetic and copies ran while one was open for 5% of the time, Pallas kernels for 0%

commit v1 on v0

v1 whole, which is shorter than its diff:
```python
import functools
import math

import jax
import jax.numpy as jnp
from jax import lax
from jax.experimental import pallas as pl
from jax.experimental.pallas import tpu as pltpu
from jax.sharding import PartitionSpec as P

HEAD_SIZE = 128
LANES = 128
BLOCK_KEYS = 512
EXP2_SCALE = 168.0 ** (-0.5) * math.log2(math.e)
MASKED = -1e30


def nt_dot(a, b):
    return lax.dot_general(a, b, (((1,), (1,)), ((), ())), preferred_element_type=jnp.float32)


def kernel(
    devices, heads, group, own, block,
    q_hbm, k_hbm, v_hbm, fk_hbm, fv_hbm, out_ref,
    qbuf, kbuf, vbuf, fkbuf, fvbuf, scores, fresh_scores, visible,
    part_max, full_max, part_sum, acc, obuf, rbuf, mlbuf, rmlbuf,
    q_sem, k_sem, v_sem, fk_sem, fv_sem,
    gather_send, gather_recv, relay_send, relay_recv,
    o_send, o_recv, ml_send, ml_recv,
):
    pairs = devices // 2
    each = group * own
    rows = devices * each
    count = kbuf.shape[1] // block
    me = lax.axis_index("ctx")
    core, pair = lax.rem(me, 2), lax.div(me, 2)
    my_slot = core * pairs + pair

    def q_copy(h, g):
        columns = pl.ds((h * group + g) * HEAD_SIZE, HEAD_SIZE)
        return pltpu.make_async_copy(
            q_hbm.at[:, columns], qbuf.at[h, core, pair, pl.ds(g * own, own)], q_sem.at[h, g]
        )

    def head_columns(h):
        return pl.ds(pl.multiple_of(h * HEAD_SIZE, HEAD_SIZE), HEAD_SIZE)

    def k_copy(h):
        return pltpu.make_async_copy(k_hbm.at[:, head_columns(h)], kbuf.at[h], k_sem.at[h])

    def v_copy(h):
        return pltpu.make_async_copy(v_hbm.at[:, head_columns(h)], vbuf.at[h], v_sem.at[h])

    def fk_copy(h):
        return pltpu.make_async_copy(
            fk_hbm.at[:, head_columns(h)], fkbuf.at[h, pl.ds(0, own)], fk_sem.at[h]
        )

    def fv_copy(h):
        return pltpu.make_async_copy(
            fv_hbm.at[:, head_columns(h)], fvbuf.at[h, pl.ds(0, own)], fv_sem.at[h]
        )

    for h in range(heads):
        for g in range(group):
            q_copy(h, g).start()

    barrier = pltpu.get_barrier_semaphore()

    def greet(step, _):
        peer = lax.rem(me + step, devices)
        pl.semaphore_signal(
            barrier, inc=1, device_id={"ctx": peer}, device_id_type=pl.DeviceIdType.MESH
        )
        return 0

    lax.fori_loop(1, devices, greet, 0)
    fkbuf[:, own:, :] = jnp.zeros((heads, LANES - own, HEAD_SIZE), fkbuf.dtype)
    fvbuf[:, own:, :] = jnp.zeros((heads, LANES - own, HEAD_SIZE), fvbuf.dtype)
    for h in range(heads):
        fk_copy(h).start()
        k_copy(h).start()
        fv_copy(h).start()
        v_copy(h).start()

    key_lane = lax.broadcasted_iota(jnp.int32, (own, LANES), 1)
    key_pos = me * own + key_lane
    token = lax.broadcasted_iota(jnp.int32, (own, LANES), 0)
    for slot in range(devices):
        device = (slot % pairs) * 2 + slot // pairs
        seen = jnp.where((key_lane < own) & (key_pos <= device * own + token), 0.0, MASKED)
        for g in range(group):
            visible[pl.ds(slot * each + g * own, own), :] = seen

    for h in range(heads):
        for g in range(group):
            q_copy(h, g).wait()
    pl.semaphore_wait(barrier, devices - 1)

    def gather_copy(h, peer_pair):
        mine = qbuf.at[h, core, pair]
        return pltpu.make_async_remote_copy(
            src_ref=mine, dst_ref=mine, send_sem=gather_send.at[h], recv_sem=gather_recv.at[h],
            device_id={"ctx": peer_pair * 2 + core}, device_id_type=pl.DeviceIdType.MESH,
        )

    def gather_head(h, _):
        def send(step, _):
            gather_copy(h, lax.rem(pair + step, pairs)).start()
            return 0

        return lax.fori_loop(1, pairs, send, 0)

    lax.fori_loop(0, heads, gather_head, 0)

    def relay_copy(h):
        mine = qbuf.at[h, core]
        return pltpu.make_async_remote_copy(
            src_ref=mine, dst_ref=mine, send_sem=relay_send.at[h], recv_sem=relay_recv.at[h],
            device_id={"ctx": pair * 2 + 1 - core}, device_id_type=pl.DeviceIdType.MESH,
        )

    def gather_blocks(h, sem):
        blocks = qbuf.at[h, core, pl.ds(0, pairs - 1)]
        return pltpu.make_async_copy(blocks, blocks, sem.at[h])

    def relay(h):
        gather_blocks(h, gather_recv).wait()
        relay_copy(h).start()

    def queries_of(h):
        return qbuf[h].reshape(rows, HEAD_SIZE)

    def scores_open(h):
        relay_copy(h).wait_recv()
        fk_copy(h).wait()
        k_copy(h).wait()
        s = nt_dot(queries_of(h), fkbuf[h]) + visible[...]
        s = jnp.where(visible[...] < 0.0, MASKED, s)
        fresh_scores[lax.rem(h, 2)] = s
        part_max[...] = s

    def scores_block(h, c):
        keys = kbuf[h, pl.ds(pl.multiple_of(c * block, block), block), :]
        s = nt_dot(queries_of(h), keys)
        scores[lax.rem(h, 2), c] = s
        top = part_max[...]
        for i in range(block // LANES):
            top = jnp.maximum(top, s[:, i * LANES:(i + 1) * LANES])
        part_max[...] = top

    def scores_close():
        full_max[...] = jnp.broadcast_to(
            jnp.max(part_max[...], axis=1, keepdims=True), full_max.shape
        )

    def values_open(h):
        fv_copy(h).wait()
        v_copy(h).wait()
        p = jnp.exp2((fresh_scores[lax.rem(h, 2)] - full_max[...]) * EXP2_SCALE)
        part_sum[...] = p
        acc[...] = jnp.dot(
            p.astype(jnp.bfloat16), fvbuf[h], preferred_element_type=jnp.float32
        )

    def values_block(h, c):
        top = full_max[...]
        total = part_sum[...]
        pieces = []
        for i in range(block // LANES):
            s = scores[lax.rem(h, 2), c, :, i * LANES:(i + 1) * LANES]
            p = jnp.exp2((s - top) * EXP2_SCALE)
            total = total + p
            pieces.append(p.astype(jnp.bfloat16))
        part_sum[...] = total
        values = vbuf[h, pl.ds(pl.multiple_of(c * block, block), block), :]
        acc[...] += jnp.dot(
            jnp.concatenate(pieces, axis=1), values, preferred_element_type=jnp.float32
        )

    lane = lax.broadcasted_iota(jnp.int32, (each, LANES), 1)
    sub = lax.broadcasted_iota(jnp.int32, (each, LANES), 0)

    def o_copy(h, slot):
        peer = lax.rem(slot, pairs) * 2 + lax.div(slot, pairs)
        return pltpu.make_async_remote_copy(
            src_ref=obuf.at[h, slot], dst_ref=rbuf.at[h, my_slot],
            send_sem=o_send.at[h], recv_sem=o_recv.at[h],
            device_id={"ctx": peer}, device_id_type=pl.DeviceIdType.MESH,
        )

    def ml_copy(h, slot):
        peer = lax.rem(slot, pairs) * 2 + lax.div(slot, pairs)
        return pltpu.make_async_remote_copy(
            src_ref=mlbuf.at[h, slot], dst_ref=rmlbuf.at[h, my_slot],
            send_sem=ml_send.at[h], recv_sem=ml_recv.at[h],
            device_id={"ctx": peer}, device_id_type=pl.DeviceIdType.MESH,
        )

    def values_close(h):
        total = jnp.sum(part_sum[...], axis=1, keepdims=True)
        out = (acc[...] / total).astype(jnp.bfloat16)
        obuf[h] = out.reshape(devices, each, HEAD_SIZE)
        for slot in range(devices):
            span = slice(slot * each, (slot + 1) * each)
            tops = jnp.where(lane == sub, full_max[span, :], 0.0)
            sums = jnp.where(lane == sub + each, jnp.broadcast_to(total[span], tops.shape), 0.0)
            mlbuf[h, slot] = jnp.sum(tops + sums, axis=0, keepdims=True)
        rbuf[h, my_slot] = obuf[h, my_slot]
        rmlbuf[h, my_slot] = mlbuf[h, my_slot]

    def send_out(h):
        def send(step, _):
            slot = lax.rem(my_slot + step, devices)
            ml_copy(h, slot).start()
            o_copy(h, slot).start()
            return 0

        lax.fori_loop(1, devices, send, 0)

    def o_blocks(ref, h, sem):
        blocks = ref.at[h, pl.ds(0, devices - 1)]
        return pltpu.make_async_copy(blocks, blocks, sem.at[h])

    def combine(h):
        o_blocks(rmlbuf, h, ml_recv).wait()
        o_blocks(rbuf, h, o_recv).wait()
        ml = rmlbuf[h, :, 0, :]
        tops, sums = ml[:, :each], ml[:, each:2 * each]
        weights = jnp.exp2((tops - jnp.max(tops, axis=0, keepdims=True)) * EXP2_SCALE) * sums
        weights = weights / jnp.sum(weights, axis=0, keepdims=True)
        diagonal = lax.broadcasted_iota(jnp.int32, (each, each), 0) == lax.broadcasted_iota(
            jnp.int32, (each, each), 1
        )
        result = jnp.zeros((each, HEAD_SIZE), jnp.float32)
        for slot in range(devices):
            row = jnp.broadcast_to(weights[slot:slot + 1, :], (each, each))
            column = jnp.sum(jnp.where(diagonal, row, 0.0), axis=1, keepdims=True)
            result = result + column * rbuf[h, slot].astype(jnp.float32)
        for g in range(group):
            columns = pl.ds(pl.multiple_of((h * group + g) * HEAD_SIZE, HEAD_SIZE), HEAD_SIZE)
            out_ref[:, columns] = result[g * own:(g + 1) * own].astype(out_ref.dtype)

    def loop(body):
        def step(c, _):
            body(c)
            return 0

        lax.fori_loop(0, count, step, 0)

    lag = 3
    relay(0)
    if heads > 1:
        relay(1)
    scores_open(0)
    loop(lambda c: scores_block(0, c))
    scores_close()

    def head_step(h, _):
        @pl.when(h + 1 < heads)
        def _():
            relay(h + 1)

        values_open(h - 1)
        scores_open(h)

        def both(c):
            values_block(h - 1, c)
            scores_block(h, c)

        loop(both)
        values_close(h - 1)
        scores_close()
        send_out(h - 1)

        @pl.when(h > lag)
        def _():
            combine(h - 1 - lag)

        return 0

    lax.fori_loop(1, heads, head_step, 0)
    last = heads - 1
    values_open(last)
    loop(lambda c: values_block(last, c))
    values_close(last)
    send_out(last)
    lax.fori_loop(max(0, heads - 1 - lag), heads, lambda h, _: (combine(h), 0)[1], 0)

    def drain(h, _):
        gather_blocks(h, gather_send).wait()
        relay_copy(h).wait_send()
        o_blocks(mlbuf, h, ml_send).wait()
        o_blocks(obuf, h, o_send).wait()
        return 0

    lax.fori_loop(0, heads, drain, 0)


def solution(mesh):
    devices = mesh.shape["ctx"]

    def shards(queries, cache_keys, prefix_values, incoming_keys, incoming_values):
        own = queries.shape[0]
        heads = cache_keys.shape[1] // HEAD_SIZE
        group = queries.shape[1] // cache_keys.shape[1]
        depth = cache_keys.shape[0]
        each = group * own
        rows = devices * each
        block = min(BLOCK_KEYS, depth)
        bf16, f32 = jnp.bfloat16, jnp.float32
        dma = pltpu.SemaphoreType.DMA
        return pl.pallas_call(
            functools.partial(kernel, devices, heads, group, own, block),
            out_shape=jax.ShapeDtypeStruct(queries.shape, queries.dtype),
            in_specs=[pl.BlockSpec(memory_space=pl.ANY)] * 5,
            out_specs=pl.BlockSpec(memory_space=pltpu.VMEM),
            scratch_shapes=[
                pltpu.VMEM((heads, 2, devices // 2, each, HEAD_SIZE), bf16),
                pltpu.VMEM((heads, depth, HEAD_SIZE), bf16),
                pltpu.VMEM((heads, depth, HEAD_SIZE), bf16),
                pltpu.VMEM((heads, LANES, HEAD_SIZE), bf16),
                pltpu.VMEM((heads, LANES, HEAD_SIZE), bf16),
                pltpu.VMEM((2, depth // block, rows, block), f32),
                pltpu.VMEM((2, rows, LANES), f32),
                pltpu.VMEM((rows, LANES), f32),
                pltpu.VMEM((rows, LANES), f32),
                pltpu.VMEM((rows, LANES), f32),
                pltpu.VMEM((rows, LANES), f32),
                pltpu.VMEM((rows, HEAD_SIZE), f32),
                pltpu.VMEM((heads, devices, each, HEAD_SIZE), bf16),
                pltpu.VMEM((heads, devices, each, HEAD_SIZE), bf16),
                pltpu.VMEM((heads, devices, 1, LANES), f32),
                pltpu.VMEM((heads, devices, 1, LANES), f32),
                dma((heads, group)), dma((heads,)), dma((heads,)), dma((heads,)), dma((heads,)),
                dma((heads,)), dma((heads,)), dma((heads,)), dma((heads,)),
                dma((heads,)), dma((heads,)), dma((heads,)), dma((heads,)),
            ],
            compiler_params=pltpu.CompilerParams(
                collective_id=0, has_side_effects=True, vmem_limit_bytes=60 * 1024 * 1024
            ),
        )(queries, cache_keys, prefix_values, incoming_keys, incoming_values)

    spec = P("ctx", "head")
    return jax.shard_map(
        shards, mesh=mesh, in_specs=(spec,) * 5, out_specs=spec, check_vma=False
    )
```

time: 409 us -> 60.3 us (0.15)
  waiting for transfers between devices: 100 us -> 0 us
  blocking collectives: 99.3 us -> 0 us
  matrix products: 92.7 us -> 0 us
  Pallas kernels: 0 us -> 58.6 us
  other arithmetic: 52.5 us -> 0 us
  local copies, waits for them, and re-layouts: 49 us -> 1.47 us
  between operations: 13.3 us -> 0.01 us
    dot_general x34 -> x0, matrix products: 92.7 us -> none  [the longest x16 61.9 us: prefix_step(): jnp.einsum('qhgd,khd->hgqk', query_heads, block_keys, preferred_element_t...]
    reduce_scatter x1 -> x0, waiting for transfers between devices: 63.6 us -> none  [shards(): lax.psum_scatter(out_acc * rescale[..., None], 'ctx', scatter_dimension=2...]
    pmax x1 -> x0, blocking collectives: 59.7 us -> none  [shards(): top_max = lax.pmax(row_max, 'ctx')]
    pallas_call x0 -> x1, Pallas kernels: none -> 58.6 us  [shards(): pl.pallas_call(functools.partial(kernel, devices, heads, group, own, bloc...]
    reduce_sum x17 -> x0, other arithmetic: 49.4 us -> none  [the longest x16 49.2 us: prefix_step(): row_sum = row_sum * decay + jnp.sum(probs, axis=-1)]
    all_gather x2 -> x0, blocking collectives: 39.7 us -> none  [the longest x1 21 us: shards(): lax.all_gather(incoming_values, 'ctx', axis=0, tiled=True)]
    all_gather x1 -> x0, waiting for transfers between devices: 25.2 us -> none  [shards(): gathered = lax.all_gather(queries, 'ctx', axis=0, tiled=True)]
    dynamic_slice x16 -> x0, local copies, waits for them, and re-layouts: 20.4 us -> none  [shards(): (out_acc, row_max, row_sum), _ = lax.scan(prefix_step, init, blocks)]
  transfers between devices with their start and end apart: 3 -> 0, of which waited for: 3 -> 0; matrix products, arithmetic and copies ran while one was open for 5% -> 0% of each run, Pallas kernels for 0% -> 0%
where the time goes in v1:
time: 60.3 us; the launch traced here: 60.1 us
  Pallas kernels  58.6 us (97%)
  local copies, waits for them, and re-layouts  1.47 us (2%)
    pallas_call x1, Pallas kernels, shards(): pl.pallas_call(functools.partial(kernel, devices, heads, group, own, bloc...  58.6 us
    unnamed x1, local copies, waits for them, and re-layouts  1.47 us

profile of v1, /device:TPU:0, one launch (start us, length us, event | category | flops | bytes accessed | tf_op | source)
XLA Modules:
  0.0 60.1 jit_solution(3671491755750369343)
XLA Ops:
  0.0 58.6 %shard_map.55 = bf16[16,2048]{1,0:T(8,128)(2,1)} custom-call(bf16[16,2048]{1,0:T(8,128)(2,1)} %q_hbm.1, bf16[4096,1024]{1,0:T(8,128)(2,1)} %k_hbm.1, bf16[4096,1024]{1,0:T(8,128)(2,1)} %v_hbm.1, bf16[16,1024]{1,0:T(8,128)(2,1)} %fk_hbm.1, bf16[16,1024]{1,0:T(8,128)(2,1)} %fv_hbm.1), custom_call_target="tpu_custom_call" | custom-call | tf_op jit(solution)/shard_map/pallas_call | solution.py:313
  58.6 1.5 %copy.7 = bf16[16,2048]{1,0:T(8,128)(2,1)} copy(bf16[16,2048]{1,0:T(8,128)(2,1)} %shard_map.55) | data formatting | bytes 131072

commit v2 on v1

--- a/solution.py
+++ b/solution.py
@@ -10,7 +10,7 @@
 
 HEAD_SIZE = 128
 LANES = 128
-BLOCK_KEYS = 512
+BLOCK_KEYS = 2048
 EXP2_SCALE = 168.0 ** (-0.5) * math.log2(math.e)
 MASKED = -1e30
 
@@ -22,7 +22,7 @@
 def kernel(
     devices, heads, group, own, block,
     q_hbm, k_hbm, v_hbm, fk_hbm, fv_hbm, out_ref,
-    qbuf, kbuf, vbuf, fkbuf, fvbuf, scores, fresh_scores, visible,
+    qbuf, kbuf, vbuf, fkbuf, fvbuf, scores_even, scores_odd, fresh_scores, visible,
     part_max, full_max, part_sum, acc, obuf, rbuf, mlbuf, rmlbuf,
     q_sem, k_sem, v_sem, fk_sem, fv_sem,
     gather_send, gather_recv, relay_send, relay_recv,
@@ -131,6 +131,8 @@
     def queries_of(h):
         return qbuf[h].reshape(rows, HEAD_SIZE)
 
+    score_slots = (scores_even, scores_odd)
+
     def scores_open(h):
         relay_copy(h).wait_recv()
         fk_copy(h).wait()
@@ -140,10 +142,10 @@
         fresh_scores[lax.rem(h, 2)] = s
         part_max[...] = s
 
-    def scores_block(h, c):
+    def scores_block(h, c, parity):
         keys = kbuf[h, pl.ds(pl.multiple_of(c * block, block), block), :]
         s = nt_dot(queries_of(h), keys)
-        scores[lax.rem(h, 2), c] = s
+        score_slots[parity][c] = s
         top = part_max[...]
         for i in range(block // LANES):
             top = jnp.maximum(top, s[:, i * LANES:(i + 1) * LANES])
@@ -163,12 +165,12 @@
             p.astype(jnp.bfloat16), fvbuf[h], preferred_element_type=jnp.float32
         )
 
-    def values_block(h, c):
+    def values_block(h, c, parity):
         top = full_max[...]
         total = part_sum[...]
         pieces = []
         for i in range(block // LANES):
-            s = scores[lax.rem(h, 2), c, :, i * LANES:(i + 1) * LANES]
+            s = score_slots[parity][c, :, i * LANES:(i + 1) * LANES]
             p = jnp.exp2((s - top) * EXP2_SCALE)
             total = total + p
             pieces.append(p.astype(jnp.bfloat16))
@@ -253,10 +255,10 @@
     if heads > 1:
         relay(1)
     scores_open(0)
-    loop(lambda c: scores_block(0, c))
+    loop(lambda c: scores_block(0, c, 0))
     scores_close()
 
-    def head_step(h, _):
+    def head_step(h, parity):
         @pl.when(h + 1 < heads)
         def _():
             relay(h + 1)
@@ -265,8 +267,8 @@
         scores_open(h)
 
         def both(c):
-            values_block(h - 1, c)
-            scores_block(h, c)
+            values_block(h - 1, c, 1 - parity)
+            scores_block(h, c, parity)
 
         loop(both)
         values_close(h - 1)
@@ -277,12 +279,17 @@
         def _():
             combine(h - 1 - lag)
 
+    def two_heads(step, _):
+        head_step(1 + 2 * step, 1)
+        head_step(2 + 2 * step, 0)
         return 0
 
-    lax.fori_loop(1, heads, head_step, 0)
+    lax.fori_loop(0, (heads - 1) // 2, two_heads, 0)
+    if heads % 2 == 0:
+        head_step(heads - 1, 1)
     last = heads - 1
     values_open(last)
-    loop(lambda c: values_block(last, c))
+    loop(lambda c: values_block(last, c, last % 2))
     values_close(last)
     send_out(last)
     lax.fori_loop(max(0, heads - 1 - lag), heads, lambda h, _: (combine(h), 0)[1], 0)
@@ -321,7 +328,8 @@
                 pltpu.VMEM((heads, depth, HEAD_SIZE), bf16),
                 pltpu.VMEM((heads, LANES, HEAD_SIZE), bf16),
                 pltpu.VMEM((heads, LANES, HEAD_SIZE), bf16),
-                pltpu.VMEM((2, depth // block, rows, block), f32),
+                pltpu.VMEM((depth // block, rows, block), f32),
+                pltpu.VMEM((depth // block, rows, block), f32),
                 pltpu.VMEM((2, rows, LANES), f32),
                 pltpu.VMEM((rows, LANES), f32),
                 pltpu.VMEM((rows, LANES), f32),

time: 60.3 us -> 52.2 us (0.87)
  Pallas kernels: 58.6 us -> 50.5 us
    pallas_call x1, Pallas kernels: 58.6 us -> 50.5 us  [shards(): pl.pallas_call(functools.partial(kernel, devices, heads, group, own, bloc...]
where the time goes in v2:
time: 52.2 us; the launch traced here: 52 us
  Pallas kernels  50.5 us (97%)
  local copies, waits for them, and re-layouts  1.47 us (3%)
    pallas_call x1, Pallas kernels, shards(): pl.pallas_call(functools.partial(kernel, devices, heads, group, own, bloc...  50.5 us
    unnamed x1, local copies, waits for them, and re-layouts  1.47 us

profile of v2, /device:TPU:0, one launch (start us, length us, event | category | flops | bytes accessed | tf_op | source)
XLA Modules:
  0.0 52.0 jit_solution(9549885048160516984)
XLA Ops:
  0.0 50.5 %shard_map.55 = bf16[16,2048]{1,0:T(8,128)(2,1)} custom-call(bf16[16,2048]{1,0:T(8,128)(2,1)} %q_hbm.1, bf16[4096,1024]{1,0:T(8,128)(2,1)} %k_hbm.1, bf16[4096,1024]{1,0:T(8,128)(2,1)} %v_hbm.1, bf16[16,1024]{1,0:T(8,128)(2,1)} %fk_hbm.1, bf16[16,1024]{1,0:T(8,128)(2,1)} %fv_hbm.1), custom_call_target="tpu_custom_call" | custom-call | tf_op jit(solution)/shard_map/pallas_call | solution.py:320
  50.5 1.5 %copy.7 = bf16[16,2048]{1,0:T(8,128)(2,1)} copy(bf16[16,2048]{1,0:T(8,128)(2,1)} %shard_map.55) | data formatting | bytes 131072
